TPU v7x, 32 devices: a whole 2x2x4 slice. The times are simulated.
32 devices in a mesh: gx: 16 (over z, x, core), ta: 2 (over y).
Axes of the slice: x: 2, y: 2, z: 4, core: 2. Of those that a mesh axis runs over, the one named last changes fastest.
Arguments:
- master_flat: float32 [8388608], P(('gx', 'ta')), may hold values from -6 to 6
Outputs:
- serving_weight: bfloat16 [1, 8192, 1024], P(None, None, 'ta')
- channel_scale: float32 [1, 1024], P(None, 'ta')
All inputs are finite; a program needn't handle non-finite values.
Results may differ from a plain program's by a relative error of at most 0.015.
Values may be sent and summed in bfloat16 or wider, within the bound.
A program may use at most 64 MiB of HBM per device.

v0:
```python
import jax
import jax.numpy as jnp
from jax import lax
from jax.sharding import PartitionSpec as P

D = 8192
KVH = 8
HEAD = 128
LAYERS = 1


def relayout(shard):
    regrouped = lax.all_to_all(shard, "ta", split_axis=1, concat_axis=0, tiled=True)
    complete = lax.all_gather(regrouped, "gx", axis=0, tiled=True)
    return complete.reshape(LAYERS, D, -1)


def shards(master_flat):
    kv_width = KVH * HEAD
    row_count = master_flat.shape[0] // kv_width
    rounded = master_flat.reshape(row_count, kv_width).astype(jnp.bfloat16)
    complete = relayout(rounded)
    widened = complete.astype(jnp.float32)
    channel_scale = jnp.max(jnp.abs(widened), axis=1)
    serving_weight = (widened / channel_scale[:, None, :]).astype(jnp.bfloat16)
    return (serving_weight, channel_scale)


def solution(mesh):
    in_specs = (P(("gx", "ta")),)
    out_specs = (P(None, None, "ta"), P(None, "ta"))
    return jax.shard_map(shards, mesh=mesh, in_specs=in_specs, out_specs=out_specs, check_vma=False)
```

profile of v0, /device:TPU:1, one launch (start us, length us, event | category | flops | bytes accessed | tf_op | source)
XLA Modules:
  0.0 116.1 jit_solution(6480745869654195963)
XLA Ops:
  7.2 0.0 all-gather.2.cloned.1.call-start
  7.2 1.3 %convert_element_type.17 = bf16[262144]{0:T(1024)(128)(2,1)S(1)} convert(f32[262144]{0:T(1024)} %param.1) | non-fusion elementwise | flops 262144 | bytes 1572864 | tf_op jit(solution)/shard_map/convert_element_type | solution.py:21
  8.5 0.2 convert_element_type.18
  8.7 0.1 copy.4
  8.8 11.4 %all_to_all.16 = bf16[256,2,512]{2,0,1:T(8,128)(2,1)} all-to-all(bf16[256,2,512]{2,0,1:T(8,128)(2,1)S(1)} %copy.4), channel_id=1, replica_groups=mesh['gx'=16,'ta'=2] {'ta'}, dimensions={1} | all-to-all | bytes 1048576 | tf_op jit(solution)/shard_map/all_to_all | solution.py:13
  20.1 0.0 all-gather.2.cloned.1.call-update
  20.1 76.3 %all-gather.2.cloned.1.call-done = bf16[8192,512]{1,0:T(8,128)(2,1)} async-done(((bf16[512,512]{1,0:T(8,128)(2,1)}), bf16[8192,512]{1,0:T(8,128)(2,1)}) %all-gather.2.cloned.1.call-update) | async-done | bytes 8388624 | tf_op jit(solution)/shard_map/all_gather | solution.py:14
  96.5 4.2 %fusion = f32[512]{0:T(512)S(1)} fusion(bf16[8192,512]{1,0:T(8,128)(2,1)} %all-gather.2.cloned.1.call-done), kind=kLoop, calls=%fused_computation.2 | loop fusion | flops 12582400 | bytes 8390656 | tf_op jit(solution)/shard_map/reduce_max | solution.py:24
  100.7 0.0 copy-start
  100.7 8.5 %fusion.2 = bf16[1,8192,512]{2,1,0:T(8,128)(2,1)} fusion(bf16[8192,512]{1,0:T(8,128)(2,1)} %all-gather.2.cloned.1.call-done, f32[512]{0:T(512)S(1)} %fusion), kind=kLoop, calls=%fused_computation.4 | loop fusion | flops 12582912 | bytes 16779264 | tf_op jit(solution)/shard_map/convert_element_type | solution.py:25
  109.2 0.0 copy-done
Async XLA Ops:
  7.2 89.3 %all-gather.2.cloned.1.call-start = ((), (), s32[]{:S(2)}) async-start(), calls=%async_computation.1 | async-start | bytes 8912896 | tf_op jit(solution)/shard_map/all_gather | solution.py:14
  100.7 8.5 %copy-start = (f32[512]{0:T(512)}, f32[512]{0:T(512)S(1)}, u32[]{:S(2)}) copy-start(f32[512]{0:T(512)S(1)} %fusion) | copy-start | bytes 6148
Sparse Core Ops, SparseCore 0:
  20.3 76.1 all-gather.1
where the time goes:
time: 117 us; the launch traced here: 116 us
  waiting for transfers between devices  76.4 us (65%)
  between operations  14.1 us (12%)
  other arithmetic  14 us (12%)
  blocking collectives  11.4 us (10%)
    all_gather x1, waiting for transfers between devices, relayout(): complete = lax.all_gather(regrouped, 'gx', axis=0, tiled=True)  76.3 us
    all_to_all x1, blocking collectives, relayout(): lax.all_to_all(shard, 'ta', split_axis=1, concat_axis=0, tiled=True)  11.4 us
    convert_element_type x1, other arithmetic, shards(): serving_weight = (widened / channel_scale[:, None, :]).astype(jnp.bfloat16)  8.52 us
    reduce_max x1, other arithmetic, shards(): channel_scale = jnp.max(jnp.abs(widened), axis=1)  4.21 us
  transfers between devices with their start and end apart: 1, of which 1 were waited for; matrix products, arithmetic and copies ran while one was open for 0% of the time, Pallas kernels for 0%

commit v1 on v0

v1 whole, which is shorter than its diff:
```python
import functools

import jax
import jax.numpy as jnp
from jax import lax
from jax.experimental import pallas as pl
from jax.experimental.pallas import tpu as pltpu
from jax.sharding import PartitionSpec as P

D = 8192
KVH = 8
HEAD = 128
LAYERS = 1
LANES = 128
CORES = 2
MESH = pl.DeviceIdType.MESH


def ring_order(mesh, chips):
    where = [getattr(d, "coords", None) for d in mesh.devices[::CORES, 0]]
    wide = 1
    if all(w is not None for w in where) and chips > 2:
        moved = [a != b for a, b in zip(where[0], where[1])].index(True)
        wide = next((c for c in range(1, chips) if where[c][moved] == where[0][moved]), chips)
    tall = chips // wide
    if wide == 1 or wide == chips or tall % 2:
        return list(range(chips))
    order = [0]
    for a in range(tall):
        columns = range(1, wide) if a % 2 == 0 else range(wide - 1, 0, -1)
        order += [a * wide + b for b in columns]
    return order + [a * wide for a in range(tall - 1, 0, -1)]


def pick(table, index):
    found = jnp.int32(table[0])
    for at in range(1, len(table)):
        found = jnp.where(index == at, jnp.int32(table[at]), found)
    return found


def kernel(n, t, order, splits, x_ref, out_ref, scale_ref,
           gath, loc, top, tops, cw_send, cw_recv, cc_send, cc_recv, dd_send, dd_recv,
           ta_send, ta_recv, top_send, top_recv):
    chips = n // CORES
    rows, width = gath.shape
    blocks = width // LANES
    piece = loc.shape[1]
    unit = piece * t
    chunk = piece // splits
    count = t * splits
    lines = t * blocks
    total = n * t

    gx, ta = lax.axis_index("gx"), lax.axis_index("ta")
    me = gx * t + ta
    chip, core = gx // CORES, lax.rem(gx, CORES)
    place = [order.index(c) for c in range(chips)]
    at = pick(place, chip)

    barrier = pltpu.get_barrier_semaphore()

    def greet(k, carry):
        other = lax.rem(me + k, total)
        pl.semaphore_signal(barrier, inc=1, device_id=(other // t, lax.rem(other, t)), device_id_type=MESH)
        return carry

    lax.fori_loop(1, total, greet, 0)

    best = None
    for r in range(lines):
        block = x_ref[pl.ds(r, piece, stride=lines), :].astype(jnp.bfloat16)
        loc[r // blocks, :, (r % blocks) * LANES:(r % blocks + 1) * LANES] = block
        high = jnp.max(jnp.abs(block.astype(jnp.float32)), axis=0, keepdims=True)
        top[r // blocks, r % blocks:r % blocks + 1, :] = high

    ring = {
        1: (cw_send, cw_recv, pick(order, lax.rem(at + 1, chips))),
        -1: (cc_send, cc_recv, pick(order, lax.rem(at + chips - 1, chips))),
    }
    reach = {
        1: [chips // 2 if j < count // 2 else chips - 1 - chips // 2 for j in range(count)],
        -1: [chips - 1 - chips // 2 if j < count // 2 else chips // 2 for j in range(count)],
    }

    def start_of(chip_at, of_core, j):
        inner = lax.rem(ta * piece + j * chunk, unit)
        return pl.multiple_of((chip_at * CORES + of_core) * unit + inner, chunk)

    def source(hop, start, j):
        if hop == 0 and j < splits:
            return loc.at[ta, pl.ds(j * chunk, chunk), :]
        return gath.at[pl.ds(start, chunk), :]

    started = []

    def send(src, start, send_sem, recv_sem, device):
        copy = pltpu.make_async_remote_copy(
            src_ref=src, dst_ref=gath.at[pl.ds(start, chunk), :], send_sem=send_sem, recv_sem=recv_sem,
            device_id=device, device_id_type=MESH)
        copy.start()
        started.append(copy)

    def arrived(start, sem):
        here = gath.at[pl.ds(start, chunk), :]
        pltpu.make_async_copy(here, here, sem).wait()

    def slot(hop, j):
        return hop * count + j

    def onward(way, hop, j, start):
        if hop < reach[way][j]:
            send_sem, recv_sem, to = ring[way]
            send(source(hop, start, j), start, send_sem.at[slot(hop, j)], recv_sem.at[slot(hop, j)],
                 (to * CORES + core, ta))

    def across(way, hop, j, start):
        index = slot(hop if way > 0 else hop + chips // 2, j)
        send(source(hop, start, j), start, dd_send.at[index], dd_recv.at[index], (chip * CORES + 1 - core, ta))

    pl.semaphore_wait(barrier, total - 1)

    def tell(k, carry):
        other = lax.rem(me + k, total)
        to = lax.rem(other, t)
        pltpu.make_async_remote_copy(
            src_ref=top.at[to], dst_ref=tops.at[k - 1], send_sem=top_send, recv_sem=top_recv,
            device_id=(other // t, to), device_id_type=MESH).start()
        return carry

    lax.fori_loop(1, total, tell, 0)

    for j in range(splits):
        start = start_of(chip, core, j)
        onward(1, 0, j, start)
        onward(-1, 0, j, start)
        for k in range(1, t):
            to = lax.rem(ta + k, t)
            index = (t - k) * splits + j
            send(loc.at[to, pl.ds(j * chunk, chunk), :], start, ta_send.at[index], ta_recv.at[index], (gx, to))
    for j in range(splits):
        across(1, 0, j, start_of(chip, core, j))

    inverse = {}

    def finish(start, own_at=None):
        for_rows = chunk
        step = min(for_rows, 32)

        def some(i, carry):
            for b in range(blocks):
                lanes = slice(b * LANES, (b + 1) * LANES)
                if own_at is None:
                    value = gath[pl.ds(pl.multiple_of(start + i * step, step), step), lanes]
                else:
                    value = loc[ta, pl.ds(pl.multiple_of(own_at + i * step, step), step), lanes]
                out_ref[pl.ds(pl.multiple_of(start + i * step, step), step), lanes] = (
                    value.astype(jnp.float32) / inverse["scale"][b:b + 1, :]).astype(jnp.bfloat16)
            return carry

        lax.fori_loop(0, for_rows // step, some, 0)

    waiting = []
    peer = []

    def settle_peer(keep):
        while len(peer) > keep:
            start, index = peer.pop(0)
            arrived(start, dd_recv.at[index])
            waiting.append((start, None))

    def settle():
        if not inverse:
            return
        while waiting:
            finish(*waiting.pop(0))

    def scale():
        everyone = tops.at[pl.ds(0, total - 1)]
        pltpu.make_async_copy(everyone, everyone, top_recv).wait()
        high = top[ta]

        def more(k, high):
            return jnp.maximum(high, tops[k])

        high = lax.fori_loop(0, total - 1, more, high)
        for b in range(blocks):
            scale_ref[:, b * LANES:(b + 1) * LANES] = high[b:b + 1, :]
        inverse["scale"] = high

    def note_peer(way, hop, j, chip_at):
        peer.append((start_of(chip_at, 1 - core, j), slot(hop if way > 0 else hop + chips // 2, j)))

    for j in range(splits):
        waiting.append((start_of(chip, core, j), j * chunk))
        note_peer(1, 0, j, chip)
    for j in range(splits, count):
        start = start_of(chip, core, j)
        arrived(start, ta_recv.at[j])
        onward(1, 0, j, start)
        onward(-1, 0, j, start)
        across(1, 0, j, start)
        waiting.append((start, None))
        note_peer(1, 0, j, chip)

    for hop in range(1, chips // 2 + 1):
        left = pick(order, lax.rem(at + chips - hop, chips))
        right = pick(order, lax.rem(at + hop, chips))
        for j in range(count):
            for way, origin in ((1, left), (-1, right)):
                if hop > reach[way][j]:
                    continue
                start = start_of(origin, core, j)
                arrived(start, ring[way][1].at[slot(hop - 1, j)])
                onward(way, hop, j, start)
                across(way, hop, j, start)
                waiting.append((start, None))
                note_peer(way, hop, j, origin)
            if hop == 1 and j == 1:
                scale()
            if inverse:
                settle_peer(4)
                settle()
    if not inverse:
        scale()
    settle_peer(0)
    settle()
    for copy in started:
        copy.wait_send()
    everyone = tops.at[pl.ds(0, total - 1)]
    pltpu.make_async_copy(everyone, everyone, top_send).wait()


def shards(mesh, order, master_flat):
    n, t = mesh.shape["gx"], mesh.shape["ta"]
    kv_width = KVH * HEAD
    piece = master_flat.shape[0] // kv_width
    rows, width = piece * n * t, kv_width // t
    blocks = width // LANES
    splits = 2 if piece % 64 == 0 else 1
    count = t * splits
    chips = n // CORES
    hops = chips // 2 * count
    dma = pltpu.SemaphoreType.DMA
    out, scale = pl.pallas_call(
        functools.partial(kernel, n, t, order, splits),
        out_shape=(jax.ShapeDtypeStruct((rows, width), jnp.bfloat16), jax.ShapeDtypeStruct((1, width), jnp.float32)),
        in_specs=[pl.BlockSpec(memory_space=pltpu.VMEM)],
        out_specs=(pl.BlockSpec(memory_space=pltpu.VMEM), pl.BlockSpec(memory_space=pltpu.VMEM)),
        scratch_shapes=[
            pltpu.VMEM((rows, width), jnp.bfloat16),
            pltpu.VMEM((t, piece, width), jnp.bfloat16),
            pltpu.VMEM((t, blocks, LANES), jnp.float32),
            pltpu.VMEM((n * t, blocks, LANES), jnp.float32),
            dma((hops,)), dma((hops,)), dma((hops,)), dma((hops,)),
            dma((2 * hops + 2 * count,)), dma((2 * hops + 2 * count,)),
            dma((count,)), dma((count,)), dma, dma,
        ],
        compiler_params=pltpu.CompilerParams(
            collective_id=0, has_side_effects=True, vmem_limit_bytes=40 * 1024 * 1024),
    )(master_flat.reshape(piece * kv_width // LANES, LANES))
    return out.reshape(LAYERS, D, -1), scale.reshape(LAYERS, -1)


def solution(mesh):
    order = ring_order(mesh, mesh.shape["gx"] // CORES)
    in_specs = (P(("gx", "ta")),)
    out_specs = (P(None, None, "ta"), P(None, "ta"))
    return jax.shard_map(functools.partial(shards, mesh, order), mesh=mesh, in_specs=in_specs, out_specs=out_specs,
                         check_vma=False)
```

time: 117 us -> 65 us (0.56)
  waiting for transfers between devices: 76.4 us -> 0 us
  Pallas kernels: 0 us -> 51.8 us
  other arithmetic: 14 us -> 0 us
  between operations: 14.1 us -> 0.65 us
  local copies, waits for them, and re-layouts: 0.26 us -> 12.3 us
  blocking collectives: 11.4 us -> 0 us
    all_gather x1 -> x0, waiting for transfers between devices: 76.3 us -> none  [relayout(): complete = lax.all_gather(regrouped, 'gx', axis=0, tiled=True)]
    pallas_call x0 -> x1, Pallas kernels: none -> 51.8 us  [shards(): pl.pallas_call(functools.partial(kernel, n, t, order, splits), out_shape=...]
    unnamed x2 -> x6, local copies, waits for them, and re-layouts: 0.01 us -> 12.3 us
    all_to_all x1 -> x0, blocking collectives: 11.4 us -> none  [relayout(): lax.all_to_all(shard, 'ta', split_axis=1, concat_axis=0, tiled=True)]
    convert_element_type x2 -> x0, other arithmetic: 9.79 us -> none  [the longest x1 8.52 us: shards(): serving_weight = (widened / channel_scale[:, None, :]).astype(jnp.bfloat16)]
    reduce_max x1 -> x0, other arithmetic: 4.21 us -> none  [shards(): channel_scale = jnp.max(jnp.abs(widened), axis=1)]
  transfers between devices with their start and end apart: 1 -> 0, of which waited for: 1 -> 0; matrix products, arithmetic and copies ran while one was open for 0% -> 0% of each run, Pallas kernels for 0% -> 0%
where the time goes in v1:
time: 65 us; the launch traced here: 64.8 us
  Pallas kernels  51.8 us (80%)
  local copies, waits for them, and re-layouts  12.3 us (19%)
  between operations  0.65 us (1%)
    pallas_call x1, Pallas kernels, shards(): pl.pallas_call(functools.partial(kernel, n, t, order, splits), out_shape=...  51.8 us
    unnamed x6, local copies, waits for them, and re-layouts  12.3 us

profile of v1, /device:TPU:1, one launch (start us, length us, event | category | flops | bytes accessed | tf_op | source)
XLA Modules:
  0.0 64.8 jit_solution(14469035374976631479)
XLA Ops:
  0.6 0.0 copy-start.1
  0.6 1.2 %copy-done.1 = f32[262144]{0:T(1024)S(1)} copy-done((f32[262144]{0:T(1024)S(1)}, f32[262144]{0:T(1024)}, u32[]{:S(2)}) %copy-start.1) | copy-done | bytes 1048600
  1.9 51.8 %shard_map.30 = (bf16[8192,512]{1,0:T(8,128)(2,1)S(1)}, f32[1,512]{1,0:T(1,128)S(1)}) custom-call(f32[2048,128]{1,0:T(8,128)S(1)} %bitcast.3), custom_call_target="tpu_custom_call" | custom-call | tf_op jit(solution)/shard_map/pallas_call | solution.py:245
  53.7 0.0 copy-start
  53.7 3.2 %copy-done = bf16[8192,512]{1,0:T(8,128)(2,1)} copy-done((bf16[8192,512]{1,0:T(8,128)(2,1)}, bf16[8192,512]{1,0:T(8,128)(2,1)S(1)}, u32[]{:S(2)}) %copy-start) | copy-done | bytes 8388632
  56.9 7.3 %copy.5 = bf16[1,8192,512]{2,1,0:T(8,128)(2,1)} copy(bf16[1,8192,512]{2,1,0:T(8,128)(2,1)} %bitcast.2) | data formatting | bytes 16777216
  64.2 0.6 copy.6
Async XLA Ops:
  0.6 1.2 %copy-start.1 = (f32[262144]{0:T(1024)S(1)}, f32[262144]{0:T(1024)}, u32[]{:S(2)}) copy-start(f32[262144]{0:T(1024)} %param.1) | copy-start | bytes 3145732
  53.7 3.2 %copy-start = (bf16[8192,512]{1,0:T(8,128)(2,1)}, bf16[8192,512]{1,0:T(8,128)(2,1)S(1)}, u32[]{:S(2)}) copy-start(bf16[8192,512]{1,0:T(8,128)(2,1)S(1)} %get-tuple-element.4) | copy-start | bytes 25165828

commit v2 on v1

--- a/solution.py
+++ b/solution.py
@@ -13,6 +13,7 @@
 LAYERS = 1
 LANES = 128
 CORES = 2
+PARTS = 8
 MESH = pl.DeviceIdType.MESH
 
 
@@ -39,8 +40,8 @@
     return found
 
 
-def kernel(n, t, order, splits, x_ref, out_ref, scale_ref,
-           gath, loc, top, tops, cw_send, cw_recv, cc_send, cc_recv, dd_send, dd_recv,
+def kernel(n, t, order, splits, master_ref, out_ref, scale_ref,
+           x_ref, x_sem, gath, loc, top, tops, cw_send, cw_recv, cc_send, cc_recv, dd_send, dd_recv,
            ta_send, ta_recv, top_send, top_recv):
     chips = n // CORES
     rows, width = gath.shape
@@ -58,6 +59,8 @@
     place = [order.index(c) for c in range(chips)]
     at = pick(place, chip)
 
+    bring = pltpu.make_async_copy(master_ref, x_ref, x_sem)
+    bring.start()
     barrier = pltpu.get_barrier_semaphore()
 
     def greet(k, carry):
@@ -67,7 +70,7 @@
 
     lax.fori_loop(1, total, greet, 0)
 
-    best = None
+    bring.wait()
     for r in range(lines):
         block = x_ref[pl.ds(r, piece, stride=lines), :].astype(jnp.bfloat16)
         loc[r // blocks, :, (r % blocks) * LANES:(r % blocks + 1) * LANES] = block
@@ -231,6 +234,18 @@
     pltpu.make_async_copy(everyone, everyone, top_send).wait()
 
 
+def store(out_ref, scale_ref, out_hbm, scale_hbm, sems, scale_sem):
+    rows = out_ref.shape[0] // PARTS
+    copies = [pltpu.make_async_copy(scale_ref, scale_hbm, scale_sem)]
+    for i in range(PARTS):
+        part = pl.ds(i * rows, rows)
+        copies.append(pltpu.make_async_copy(out_ref.at[part, :], out_hbm.at[part, :], sems.at[i]))
+    for copy in copies:
+        copy.start()
+    for copy in copies:
+        copy.wait()
+
+
 def shards(mesh, order, master_flat):
     n, t = mesh.shape["gx"], mesh.shape["ta"]
     kv_width = KVH * HEAD
@@ -245,9 +260,10 @@
     out, scale = pl.pallas_call(
         functools.partial(kernel, n, t, order, splits),
         out_shape=(jax.ShapeDtypeStruct((rows, width), jnp.bfloat16), jax.ShapeDtypeStruct((1, width), jnp.float32)),
-        in_specs=[pl.BlockSpec(memory_space=pltpu.VMEM)],
+        in_specs=[pl.BlockSpec(memory_space=pltpu.HBM)],
         out_specs=(pl.BlockSpec(memory_space=pltpu.VMEM), pl.BlockSpec(memory_space=pltpu.VMEM)),
         scratch_shapes=[
+            pltpu.VMEM((piece * kv_width // LANES, LANES), jnp.float32), dma,
             pltpu.VMEM((rows, width), jnp.bfloat16),
             pltpu.VMEM((t, piece, width), jnp.bfloat16),
             pltpu.VMEM((t, blocks, LANES), jnp.float32),
@@ -259,6 +275,14 @@
         compiler_params=pltpu.CompilerParams(
             collective_id=0, has_side_effects=True, vmem_limit_bytes=40 * 1024 * 1024),
     )(master_flat.reshape(piece * kv_width // LANES, LANES))
+    out, scale = pl.pallas_call(
+        store,
+        out_shape=(jax.ShapeDtypeStruct(out.shape, out.dtype), jax.ShapeDtypeStruct(scale.shape, scale.dtype)),
+        in_specs=[pl.BlockSpec(memory_space=pltpu.VMEM)] * 2,
+        out_specs=(pl.BlockSpec(memory_space=pltpu.HBM),) * 2,
+        scratch_shapes=[dma((PARTS,)), dma],
+        compiler_params=pltpu.CompilerParams(vmem_limit_bytes=1024 * 1024),
+    )(out, scale)
     return out.reshape(LAYERS, D, -1), scale.reshape(LAYERS, -1)
 
 

time: 65 us -> 57.6 us (0.89)
  local copies, waits for them, and re-layouts: 12.3 us -> 1.22 us
  Pallas kernels: 51.8 us -> 55.6 us
    unnamed x6 -> x2, local copies, waits for them, and re-layouts: 12.3 us -> 1.22 us
    pallas_call x0 -> x1, Pallas kernels: none -> 3.38 us  [shards(): pl.pallas_call(store, out_shape=(jax.ShapeDtypeStruct(out.shape, out.dtyp...]
where the time goes in v2:
time: 57.6 us; the launch traced here: 57.4 us
  Pallas kernels  55.6 us (97%)
  local copies, waits for them, and re-layouts  1.22 us (2%)
  between operations  0.65 us (1%)
    pallas_call x1, Pallas kernels, shards(): pl.pallas_call(functools.partial(kernel, n, t, order, splits), out_shape=...  52.2 us
    pallas_call x1, Pallas kernels, shards(): pl.pallas_call(store, out_shape=(jax.ShapeDtypeStruct(out.shape, out.dtyp...  3.38 us
    unnamed x2, local copies, waits for them, and re-layouts  1.22 us

profile of v2, /device:TPU:1, one launch (start us, length us, event | category | flops | bytes accessed | tf_op | source)
XLA Modules:
  0.0 57.4 jit_solution(199471825512004166)
XLA Ops:
  0.6 0.0 copy-start
  0.6 1.2 %copy-done = f32[262144]{0:T(1024)S(1)} copy-done((f32[262144]{0:T(1024)S(1)}, f32[262144]{0:T(1024)}, u32[]{:S(2)}) %copy-start) | copy-done | bytes 1048600
  1.9 52.2 %shard_map.30 = (bf16[8192,512]{1,0:T(8,128)(2,1)S(1)}, f32[1,512]{1,0:T(1,128)S(1)}) custom-call(f32[2048,128]{1,0:T(8,128)S(1)} %bitcast.2), custom_call_target="tpu_custom_call" | custom-call | tf_op jit(solution)/shard_map/pallas_call | solution.py:260
  54.0 3.4 %shard_map.31 = (bf16[8192,512]{1,0:T(8,128)(2,1)}, f32[1,512]{1,0:T(1,128)}) custom-call(bf16[8192,512]{1,0:T(8,128)(2,1)S(1)} %get-tuple-element.6.out_ref, f32[1,512]{1,0:T(1,128)S(1)} %get-tuple-element.7.scale_ref), custom_call_target="tpu_custom_call" | custom-call | tf_op jit(solution)/shard_map/pallas_call | solution.py:278
Async XLA Ops:
  0.6 1.2 %copy-start = (f32[262144]{0:T(1024)S(1)}, f32[262144]{0:T(1024)}, u32[]{:S(2)}) copy-start(f32[262144]{0:T(1024)} %param.1) | copy-start | bytes 3145732
